TPU v7x, 8 devices: a whole 2x2x1 slice. The times are simulated.
8 devices in a mesh: pod: 1 (over z), data: 2 (over y), expert: 4 (over x, core).
Axes of the slice: x: 2, y: 2, z: 1, core: 2. Of those that a mesh axis runs over, the one named last changes fastest.
Arguments:
- x_tokens: bfloat16 [8192, 1024], P(('pod', 'data', 'expert'))
- sel_tokens: int32 [32, 256], P(('pod', 'expert'), 'data')
- gate_w: float32 [32, 256], P(('pod', 'expert'), 'data')
- w_in: bfloat16 [32, 1024, 4096], P('expert')
- w_out: bfloat16 [32, 4096, 1024], P('expert')
Outputs:
- output: bfloat16 [8192, 1024], P(('pod', 'data', 'expert'))
All inputs are finite; a program needn't handle non-finite values.
Results may differ from a plain program's by a relative error of at most 0.001.
Values are sent between devices in bfloat16 or wider.
A program may use at most 1 GiB of HBM per device.

v0:
```python
import jax
import jax.numpy as jnp
from jax import lax
from jax.sharding import PartitionSpec as P, NamedSharding


def solution(mesh):
    data_ways = mesh.shape["data"]
    expert_ways = mesh.shape["expert"]
    sources = data_ways * expert_ways
    row_spec = P(("pod", "data", "expert"), None)
    slot_spec = P(("pod", "expert"), "data")
    weight_spec = P("expert", None, None)

    def exchange(buffer):
        buffer = lax.all_to_all(buffer, "expert", 1, 1, tiled=True)
        return lax.all_to_all(buffer, "data", 0, 0, tiled=True)

    def local_fn(x_loc, sel_loc, gate_loc, w_in, w_out):
        tok_dev, d_model = x_loc.shape
        e_local, c_local = sel_loc.shape
        slots = e_local * c_local
        per_pair = 2 * slots // sources
        buf_size = sources * per_pair
        flat_sel = sel_loc.reshape(slots)
        src_dev = flat_sel // tok_dev
        src_row = flat_sel % tok_dev
        order = jnp.argsort(src_dev, stable=True)
        sorted_src = src_dev[order]
        first_pos = jnp.searchsorted(sorted_src, sorted_src, side="left")
        rank_sorted = (jnp.arange(slots) - first_pos).astype(jnp.int32)
        slot_rank = jnp.zeros(slots, jnp.int32).at[order].set(rank_sorted)
        buf_pos = src_dev * per_pair + slot_rank
        buf_slot = jnp.full(buf_size, slots, jnp.int32).at[buf_pos].set(jnp.arange(slots, dtype=jnp.int32))
        request = jnp.take(src_row, buf_slot, mode="fill", fill_value=0)
        request = exchange(request.reshape(data_ways, expert_ways, per_pair))
        served = jnp.take(x_loc, request.reshape(buf_size), axis=0)
        received = exchange(served.reshape(data_ways, expert_ways, per_pair, d_model))
        rows = jnp.take(received.reshape(buf_size, d_model), buf_pos, axis=0).reshape(e_local, c_local, d_model)
        hidden = jnp.einsum("ecd,edf->ecf", rows, w_in, preferred_element_type=jnp.float32)
        hidden = jax.nn.gelu(hidden, approximate=True).astype(jnp.bfloat16)
        expert_out = jnp.einsum("ecf,efd->ecd", hidden, w_out, preferred_element_type=jnp.float32)
        contrib = (gate_loc[:, :, None] * expert_out).astype(jnp.bfloat16).reshape(slots, d_model)
        outgoing = jnp.take(contrib, buf_slot, axis=0, mode="fill", fill_value=0)
        returned = exchange(outgoing.reshape(data_ways, expert_ways, per_pair, d_model))
        total = jax.ops.segment_sum(returned.reshape(buf_size, d_model).astype(jnp.float32), request.reshape(buf_size), num_segments=tok_dev)
        return (x_loc.astype(jnp.float32) + total).astype(jnp.bfloat16)

    return jax.shard_map(local_fn, mesh=mesh, in_specs=(row_spec, slot_spec, slot_spec, weight_spec, weight_spec), out_specs=row_spec, check_vma=False)
```

profile of v0, /device:TPU:0, one launch (start us, length us, event | category | flops | bytes accessed | tf_op | source)
XLA Modules:
  0.0 420.4 jit_solution(7323473615971358016)
XLA Ops:
  0.7 4.4 %sort.17 = (s32[1024]{0:T(1024)}, s32[1024]{0:T(1024)S(1)}) sort(s32[1024]{0:T(1024)S(1)} %get-tuple-element.103, s32[1024]{0:T(1024)S(1)} %iota.10), dimensions={0}, to_apply=%region_0.1 | sort | flops 10240 | bytes 16384 | tf_op jit(solution)/shard_map/jit(argsort)/sort | solution.py:28
  5.1 4.5 %gather_fusion.1 = s32[1024]{0:T(1024)S(1)} fusion(s32[1024]{0:T(1024)S(1)} %get-tuple-element.103, s32[1024]{0:T(1024)S(1)} %get-tuple-element.104), kind=kCustom, calls=%fused_computation.1 | custom fusion | bytes 12288 | tf_op jit(solution)/shard_map/gather | solution.py:29
  9.6 50.7 %while.25 = (s32[]{:T(128)}, u32[1024]{0:T(1024)S(1)}, u32[1024]{0:T(1024)S(1)}, s32[1024]{0:T(1024)S(1)}, s32[]{:T(128)}, /*index=5*/s32[]{:T(128)}, s32[]{}) while((s32[]{:T(128)}, u32[1024]{0:T(1024)S(1)}, u32[1024]{0:T(1024)S(1)}, s32[1024]{0:T(1024)S(1)}, s32[]{:T(128)}, /*index=5*/s32[]{:T(128)}, s32[]{}) %tuple.39), condition=%wide.region_2.3_spmd.clone, body=%wide.region_1.2_spmd.clone.sunk | while | flops 19460 | bytes 67685 | solution.py:30
  9.6 4.5 %gather_fusion = s32[1024]{0:T(1024)S(1)} fusion(s32[1024]{0:T(1024)S(1)} %get-tuple-element.152, u32[1024]{0:T(1024)S(1)} %broadcast_clamp_fusion.5), kind=kCustom, calls=%fused_computation.clone.clone.1 | custom fusion | bytes 12288 | tf_op jit(solution)/shard_map/jit(searchsorted)/jit(_searchsorted_scan_impl)/vmap(jit(_searchsorted_scan_impl))/while/body/eval_jaxpr/gather | solution.py:30
  14.3 4.5 %gather_fusion = s32[1024]{0:T(1024)S(1)} fusion(s32[1024]{0:T(1024)S(1)} %get-tuple-element.152, u32[1024]{0:T(1024)S(1)} %broadcast_clamp_fusion.5), kind=kCustom, calls=%fused_computation.clone.clone.1 | custom fusion | bytes 12288 | tf_op jit(solution)/shard_map/jit(searchsorted)/jit(_searchsorted_scan_impl)/vmap(jit(_searchsorted_scan_impl))/while/body/eval_jaxpr/gather | solution.py:30
  18.9 4.5 %gather_fusion = s32[1024]{0:T(1024)S(1)} fusion(s32[1024]{0:T(1024)S(1)} %get-tuple-element.152, u32[1024]{0:T(1024)S(1)} %broadcast_clamp_fusion.5), kind=kCustom, calls=%fused_computation.clone.clone.1 | custom fusion | bytes 12288 | tf_op jit(solution)/shard_map/jit(searchsorted)/jit(_searchsorted_scan_impl)/vmap(jit(_searchsorted_scan_impl))/while/body/eval_jaxpr/gather | solution.py:30
  23.5 4.5 %gather_fusion = s32[1024]{0:T(1024)S(1)} fusion(s32[1024]{0:T(1024)S(1)} %get-tuple-element.152, u32[1024]{0:T(1024)S(1)} %broadcast_clamp_fusion.5), kind=kCustom, calls=%fused_computation.clone.clone.1 | custom fusion | bytes 12288 | tf_op jit(solution)/shard_map/jit(searchsorted)/jit(_searchsorted_scan_impl)/vmap(jit(_searchsorted_scan_impl))/while/body/eval_jaxpr/gather | solution.py:30
  28.1 4.5 %gather_fusion = s32[1024]{0:T(1024)S(1)} fusion(s32[1024]{0:T(1024)S(1)} %get-tuple-element.152, u32[1024]{0:T(1024)S(1)} %broadcast_clamp_fusion.5), kind=kCustom, calls=%fused_computation.clone.clone.1 | custom fusion | bytes 12288 | tf_op jit(solution)/shard_map/jit(searchsorted)/jit(_searchsorted_scan_impl)/vmap(jit(_searchsorted_scan_impl))/while/body/eval_jaxpr/gather | solution.py:30
  32.7 4.5 %gather_fusion = s32[1024]{0:T(1024)S(1)} fusion(s32[1024]{0:T(1024)S(1)} %get-tuple-element.152, u32[1024]{0:T(1024)S(1)} %broadcast_clamp_fusion.5), kind=kCustom, calls=%fused_computation.clone.clone.1 | custom fusion | bytes 12288 | tf_op jit(solution)/shard_map/jit(searchsorted)/jit(_searchsorted_scan_impl)/vmap(jit(_searchsorted_scan_impl))/while/body/eval_jaxpr/gather | solution.py:30
  37.3 4.5 %gather_fusion = s32[1024]{0:T(1024)S(1)} fusion(s32[1024]{0:T(1024)S(1)} %get-tuple-element.152, u32[1024]{0:T(1024)S(1)} %broadcast_clamp_fusion.5), kind=kCustom, calls=%fused_computation.clone.clone.1 | custom fusion | bytes 12288 | tf_op jit(solution)/shard_map/jit(searchsorted)/jit(_searchsorted_scan_impl)/vmap(jit(_searchsorted_scan_impl))/while/body/eval_jaxpr/gather | solution.py:30
  41.9 4.5 %gather_fusion = s32[1024]{0:T(1024)S(1)} fusion(s32[1024]{0:T(1024)S(1)} %get-tuple-element.152, u32[1024]{0:T(1024)S(1)} %broadcast_clamp_fusion.5), kind=kCustom, calls=%fused_computation.clone.clone.1 | custom fusion | bytes 12288 | tf_op jit(solution)/shard_map/jit(searchsorted)/jit(_searchsorted_scan_impl)/vmap(jit(_searchsorted_scan_impl))/while/body/eval_jaxpr/gather | solution.py:30
  46.5 4.5 %gather_fusion = s32[1024]{0:T(1024)S(1)} fusion(s32[1024]{0:T(1024)S(1)} %get-tuple-element.152, u32[1024]{0:T(1024)S(1)} %broadcast_clamp_fusion.5), kind=kCustom, calls=%fused_computation.clone.clone.1 | custom fusion | bytes 12288 | tf_op jit(solution)/shard_map/jit(searchsorted)/jit(_searchsorted_scan_impl)/vmap(jit(_searchsorted_scan_impl))/while/body/eval_jaxpr/gather | solution.py:30
  51.2 4.5 %gather_fusion = s32[1024]{0:T(1024)S(1)} fusion(s32[1024]{0:T(1024)S(1)} %get-tuple-element.152, u32[1024]{0:T(1024)S(1)} %broadcast_clamp_fusion.5), kind=kCustom, calls=%fused_computation.clone.clone.1 | custom fusion | bytes 12288 | tf_op jit(solution)/shard_map/jit(searchsorted)/jit(_searchsorted_scan_impl)/vmap(jit(_searchsorted_scan_impl))/while/body/eval_jaxpr/gather | solution.py:30
  55.8 4.5 %gather_fusion = s32[1024]{0:T(1024)S(1)} fusion(s32[1024]{0:T(1024)S(1)} %get-tuple-element.152, u32[1024]{0:T(1024)S(1)} %broadcast_clamp_fusion.5), kind=kCustom, calls=%fused_computation.clone.clone.1 | custom fusion | bytes 12288 | tf_op jit(solution)/shard_map/jit(searchsorted)/jit(_searchsorted_scan_impl)/vmap(jit(_searchsorted_scan_impl))/while/body/eval_jaxpr/gather | solution.py:30
  60.4 4.3 %scatter_custom_fusion = s32[1024]{0:T(1024)S(1)} fusion(s32[1024]{0:T(1024)S(1)} %get-tuple-element.105, s32[1024]{0:T(1024)S(1)} %convert_subtract_fusion, s32[]{:T(128)} %constant.111.clone.1), kind=kCustom, calls=%fused_computation.62 | custom fusion | bytes 4100 | tf_op jit(solution)/shard_map/scatter | solution.py:32
  64.7 4.3 %scatter_custom_fusion.1 = s32[2048]{0:T(1024)S(1)} fusion(s32[1024]{0:T(1024)S(1)} %get-tuple-element.101, s32[1024]{0:T(1024)S(1)} %iota.12, s32[]{:T(128)} %constant.109.clone.1), kind=kCustom, calls=%fused_computation.55 | custom fusion | bytes 8196 | tf_op jit(solution)/shard_map/scatter | solution.py:34
  69.1 8.6 %gather_fusion.2 = s32[2048]{0:T(1024)S(1)} fusion(s32[1024]{0:T(1024)S(1)} %get-tuple-element.102, s32[2048]{0:T(1024)S(1)} %fusion.22), kind=kCustom, calls=%fused_computation.2 | custom fusion | bytes 24576 | tf_op jit(solution)/shard_map/jit(_take)/gather | solution.py:35
  77.8 8.2 %all_to_all.30 = s32[2,4,256]{2,0,1:T(2,128)S(1)} all-to-all(s32[2,4,256]{2,0,1:T(2,128)S(1)} %copy.17), channel_id=1, replica_groups=mesh['pod'=1,'data'=2,'expert'=4] {'expert'}, dimensions={1} | all-to-all | bytes 16384 | tf_op jit(solution)/shard_map/all_to_all | solution.py:16
  86.0 6.4 %all_to_all.31 = s32[2,4,256]{2,1,0:T(4,128)S(1)} all-to-all(s32[2,4,256]{2,1,0:T(4,128)S(1)} %copy.18), channel_id=1, replica_groups=mesh['pod'=1,'data'=2,'expert'=4] {'data'}, dimensions={0} | all-to-all | bytes 16384 | tf_op jit(solution)/shard_map/all_to_all | solution.py:17
  92.5 9.6 %gather_fusion.3 = bf16[2048,1024]{1,0:T(8,128)(2,1)} fusion(bf16[1024,1024]{1,0:T(8,128)(2,1)S(1)} %copy-done, s32[2048]{0:T(1024)S(1)} %broadcast_clamp_fusion.1), kind=kCustom, calls=%fused_computation.3 | custom fusion | bytes 8396800 | tf_op jit(solution)/shard_map/jit(_take)/gather | solution.py:37
  104.6 50.7 %all_to_all.32 = bf16[2,4,256,1024]{3,2,0,1:T(8,128)(2,1)S(1)} all-to-all(bf16[2,4,256,1024]{3,2,0,1:T(8,128)(2,1)S(1)} %copy_select_fusion.1), channel_id=1, replica_groups=mesh['pod'=1,'data'=2,'expert'=4] {'expert'}, dimensions={1} | all-to-all | bytes 8388608 | tf_op jit(solution)/shard_map/all_to_all | solution.py:16
  157.8 5.8 %all-to-all-start.3 = ((bf16[2,4,256,1024]{3,2,1,0:T(8,128)(2,1)}), bf16[2,4,256,1024]{3,2,1,0:T(8,128)(2,1)}, u32[]{:S(2)}, u32[]{:S(2)}) async-start(bf16[2,4,256,1024]{3,2,1,0:T(8,128)(2,1)} %copy.22), calls=%async_computation.3 | async-start | bytes 8388608 | tf_op jit(solution)/shard_map/all_to_all | solution.py:17
  164.1 46.2 %all-to-all-done.3 = bf16[2,4,256,1024]{3,2,1,0:T(8,128)(2,1)} async-done(((bf16[2,4,256,1024]{3,2,1,0:T(8,128)(2,1)}), bf16[2,4,256,1024]{3,2,1,0:T(8,128)(2,1)}, u32[]{:S(2)}, u32[]{:S(2)}) %all-to-all-start.3) | async-done | bytes 4194336 | tf_op jit(solution)/shard_map/all_to_all | solution.py:17
  210.3 7.7 %gather_fusion.4 = bf16[1024,1024]{1,0:T(8,128)(2,1)S(1)} fusion(bf16[2048,1024]{1,0:T(8,128)(2,1)} %bitcast.4, s32[1024]{0:T(1024)S(1)} %broadcast_clamp_fusion.2), kind=kCustom, calls=%fused_computation.4 | custom fusion | bytes 4198400 | tf_op jit(solution)/shard_map/jit(_take)/gather | solution.py:39
  218.1 29.1 %fusion.18 = f32[8,128,4096]{2,1,0:T(8,128)} fusion(bf16[8,1024,4096]{2,1,0:T(8,128)(2,1)} %param.10, bf16[8,128,1024]{2,1,0:T(8,128)(2,1)S(1)} %bitcast.44, pred[8,128]{1,0:T(8,128)(4,1)S(1)} %get-tuple-element.100), kind=kOutput, calls=%fused_computation.32 | convolution fusion | flops 8590983168 | bytes 85984256 | tf_op jit(solution)/shard_map/ecd,edf->ecf/dot_general | solution.py:40
  247.1 29.3 %multiply_convert_fusion = bf16[8,128,1024]{2,1,0:T(8,128)(2,1)S(1)} fusion(bf16[8,4096,1024]{2,1,0:T(8,128)(2,1)} %param.11, f32[8,128,4096]{2,1,0:T(8,128)} %fusion.18, f32[8,128]{1,0:T(8,128)S(1)} %copy-done.8), kind=kOutput, calls=%fused_computation.31 | convolution fusion | flops 8629780480 | bytes 85987328 | tf_op jit(solution)/shard_map/ecf,efd->ecd/dot_general | solution.py:42
  276.4 9.6 %gather_fusion.5 = bf16[2048,1024]{1,0:T(8,128)(2,1)} fusion(bf16[1024,1024]{1,0:T(8,128)(2,1)S(1)} %bitcast.43, s32[2048]{0:T(1024)S(1)} %copy-done.5), kind=kCustom, calls=%fused_computation.5 | custom fusion | bytes 8396800 | tf_op jit(solution)/shard_map/jit(_take)/gather | solution.py:44
  288.6 50.7 %all_to_all.33 = bf16[2,4,256,1024]{3,2,0,1:T(8,128)(2,1)S(1)} all-to-all(bf16[2,4,256,1024]{3,2,0,1:T(8,128)(2,1)S(1)} %copy_select_fusion), channel_id=1, replica_groups=mesh['pod'=1,'data'=2,'expert'=4] {'expert'}, dimensions={1} | all-to-all | bytes 8388608 | tf_op jit(solution)/shard_map/all_to_all | solution.py:16
  341.7 5.9 %all-to-all-start.5 = ((bf16[2,4,256,1024]{3,2,1,0:T(8,128)(2,1)}), bf16[2,4,256,1024]{3,2,1,0:T(8,128)(2,1)}, u32[]{:S(2)}, u32[]{:S(2)}) async-start(bf16[2,4,256,1024]{3,2,1,0:T(8,128)(2,1)} %copy.24), calls=%async_computation.5 | async-start | bytes 8388608 | tf_op jit(solution)/shard_map/all_to_all | solution.py:17
  350.1 44.3 %all-to-all-done.5 = bf16[2,4,256,1024]{3,2,1,0:T(8,128)(2,1)} async-done(((bf16[2,4,256,1024]{3,2,1,0:T(8,128)(2,1)}), bf16[2,4,256,1024]{3,2,1,0:T(8,128)(2,1)}, u32[]{:S(2)}, u32[]{:S(2)}) %all-to-all-start.5) | async-done | bytes 4194336 | tf_op jit(solution)/shard_map/all_to_all | solution.py:17
  394.4 22.2 %scatter_custom_fusion.2 = f32[1024,1024]{1,0:T(8,128)} fusion(f32[1024,1024]{1,0:T(8,128)} %convert_element_type.29, s32[2048]{0:T(1024)S(1)} %bitcast.49, bf16[2048,1024]{1,0:T(8,128)(2,1)} %bitcast.9), kind=kCustom, calls=%fused_computation.23 | custom fusion | flops 4194304 | bytes 8388608 | tf_op jit(solution)/shard_map/scatter-add | solution.py:46
  416.6 3.8 convert_element_type.35
  (90 shorter events, 14.0 us)
Async XLA Ops:
  9.6 55.1 %copy-start.7 = (s32[8,128]{1,0:T(8,128)S(1)}, s32[8,128]{1,0:T(8,128)}, u32[]{:S(2)}) copy-start(s32[8,128]{1,0:T(8,128)} %param.8) | copy-start | bytes 12292
  69.1 8.6 %copy-start.4 = (s32[2048]{0:T(1024)}, s32[2048]{0:T(1024)S(1)}, u32[]{:S(2)}) copy-start(s32[2048]{0:T(1024)S(1)} %fusion.22) | copy-start | bytes 24580
  69.1 23.4 %copy-start = (bf16[1024,1024]{1,0:T(8,128)(2,1)S(1)}, bf16[1024,1024]{1,0:T(8,128)(2,1)}, u32[]{:S(2)}) copy-start(bf16[1024,1024]{1,0:T(8,128)(2,1)} %param.7) | copy-start | bytes 6291460
  92.4 9.7 %copy-start.2 = (s32[2,4,256]{2,1,0:T(4,128)}, s32[2,4,256]{2,1,0:T(4,128)S(1)}, u32[]{:S(2)}) copy-start(s32[2,4,256]{2,1,0:T(4,128)S(1)} %all_to_all.31) | copy-start | bytes 24580
  157.8 52.6 %all-to-all-start.3 = ((bf16[2,4,256,1024]{3,2,1,0:T(8,128)(2,1)}), bf16[2,4,256,1024]{3,2,1,0:T(8,128)(2,1)}, u32[]{:S(2)}, u32[]{:S(2)}) async-start(bf16[2,4,256,1024]{3,2,1,0:T(8,128)(2,1)} %copy.22), calls=%async_computation.3 | async-start | bytes 8388608 | tf_op jit(solution)/shard_map/all_to_all | solution.py:17
  218.1 29.1 %copy-start.8 = (f32[8,128]{1,0:T(8,128)S(1)}, f32[8,128]{1,0:T(8,128)}, u32[]{:S(2)}) copy-start(f32[8,128]{1,0:T(8,128)} %param.9) | copy-start | bytes 12292
  247.1 29.3 %copy-start.5 = (s32[2048]{0:T(1024)S(1)}, s32[2048]{0:T(1024)}, u32[]{:S(2)}) copy-start(s32[2048]{0:T(1024)} %copy-done.4) | copy-start | bytes 24580
  276.4 9.7 %copy-start.6 = (pred[2,4,256]{2,0,1:T(4,128)(4,1)S(1)}, pred[2,4,256]{2,0,1:T(4,128)(4,1)}, u32[]{:S(2)}) copy-start(pred[2,4,256]{2,0,1:T(4,128)(4,1)} %copy.19) | copy-start | bytes 6148
  341.7 6.0 %copy-start.1 = (bf16[1024,1024]{1,0:T(8,128)(2,1)S(1)}, bf16[1024,1024]{1,0:T(8,128)(2,1)}, u32[]{:S(2)}) copy-start(bf16[1024,1024]{1,0:T(8,128)(2,1)} %param.7) | copy-start | bytes 6291460
  341.7 52.7 %all-to-all-start.5 = ((bf16[2,4,256,1024]{3,2,1,0:T(8,128)(2,1)}), bf16[2,4,256,1024]{3,2,1,0:T(8,128)(2,1)}, u32[]{:S(2)}, u32[]{:S(2)}) async-start(bf16[2,4,256,1024]{3,2,1,0:T(8,128)(2,1)} %copy.24), calls=%async_computation.5 | async-start | bytes 8388608 | tf_op jit(solution)/shard_map/all_to_all | solution.py:17
  347.6 2.5 copy-start.3
where the time goes:
time: 421 us; the launch traced here: 420 us
  blocking collectives  116 us (28%)
  local copies, waits for them, and re-layouts  104 us (25%)
  waiting for transfers between devices  90.5 us (21%)
  matrix products  58.4 us (14%)
  other arithmetic  38.9 us (9%)
  starting transfers between devices  11.7 us (3%)
    all_to_all x3, blocking collectives, exchange(): buffer = lax.all_to_all(buffer, 'expert', 1, 1, tiled=True)  110 us
    all_to_all x2, waiting for transfers between devices, exchange(): return lax.all_to_all(buffer, 'data', 0, 0, tiled=True)  90.5 us
    gather x11, local copies, waits for them, and re-layouts, local_fn(): first_pos = jnp.searchsorted(sorted_src, sorted_src, side='left')  49.8 us
    dot_general x1, matrix products, local_fn(): jnp.einsum('ecf,efd->ecd', hidden, w_out, preferred_element_type=jnp.floa...  29.3 us
    dot_general x1, matrix products, local_fn(): jnp.einsum('ecd,edf->ecf', rows, w_in, preferred_element_type=jnp.float32)  29.1 us
    scatter-add x1, other arithmetic, local_fn(): jax.ops.segment_sum(returned.reshape(buf_size, d_model).astype(jnp.float3...  22.2 us
    all_to_all x2, starting transfers between devices, exchange(): return lax.all_to_all(buffer, 'data', 0, 0, tiled=True)  11.7 us
    gather x1, local copies, waits for them, and re-layouts, local_fn(): served = jnp.take(x_loc, request.reshape(buf_size), axis=0)  9.64 us
  transfers between devices with their start and end apart: 2, of which 2 were waited for; matrix products, arithmetic and copies ran while one was open for 1% of the time, Pallas kernels for 0%

commit v1 on v0

v1 whole, which is shorter than its diff:
```python
import functools

import jax
import jax.numpy as jnp
from jax import lax
from jax.experimental import pallas as pl
from jax.experimental.pallas import tpu as pltpu
from jax.sharding import PartitionSpec as P

MESH = pl.DeviceIdType.MESH
VM = pl.BlockSpec(memory_space=pltpu.VMEM)
SM = pl.BlockSpec(memory_space=pltpu.SMEM)
ANY = pl.BlockSpec(memory_space=pl.ANY)
F32, BF16, I32 = jnp.float32, jnp.bfloat16, jnp.int32


def coords():
    return lax.axis_index("pod"), lax.axis_index("data"), lax.axis_index("expert")


def meet(peers):
    barrier = pltpu.get_barrier_semaphore()
    for peer in peers:
        pl.semaphore_signal(barrier, inc=1, device_id=peer, device_id_type=MESH)
    pl.semaphore_wait(barrier, len(peers))


def share_kernel(sel_ref, gate_ref, sel_all, gate_two, send, recv, gsem):
    pod, i, j = coords()
    peers = [(pod, lax.rem(i + di, 2), lax.rem(j + dj, 4)) for di in range(2) for dj in range(4) if (di, dj) != (0, 0)]
    meet(peers)
    me = i * 4 + j
    sel_all[me] = sel_ref[...]
    gate_two[i] = gate_ref[...]
    copies = []
    for k, peer in enumerate(peers):
        copies.append(pltpu.make_async_remote_copy(sel_ref, sel_all.at[me], send.at[k], recv.at[k], device_id=peer, device_id_type=MESH))
    copies.append(pltpu.make_async_remote_copy(gate_ref, gate_two.at[i], gsem.at[0], gsem.at[1], device_id=(pod, 1 - i, j), device_id_type=MESH))
    for c in copies:
        c.start()
    for c in copies:
        c.wait()


def share(sel, gate):
    e, c = sel.shape
    return pl.pallas_call(
        share_kernel,
        out_shape=(jax.ShapeDtypeStruct((8, e, c), I32), jax.ShapeDtypeStruct((2, e, c), F32)),
        in_specs=[VM, VM],
        out_specs=(VM, VM),
        scratch_shapes=[pltpu.SemaphoreType.DMA((7,)), pltpu.SemaphoreType.DMA((7,)), pltpu.SemaphoreType.DMA((2,))],
        compiler_params=pltpu.CompilerParams(collective_id=0, has_side_effects=True),
        name="share",
    )(sel, gate)


def route_kernel(cap_r, sel_all, gate_two, src_ref, xpos_ref, own_ref, part_ref, xrow_ref, gate_ref):
    _, i, j = coords()
    sel = jnp.concatenate([sel_all[j], sel_all[4 + j]], axis=1)
    gate = jnp.concatenate([gate_two[0], gate_two[1]], axis=1)
    half = sel // 4096
    tdev = (sel // 1024) % 4
    row = sel % 1024
    mine = half == i
    src = jnp.where(tdev == j, row, jnp.where(tdev == (j ^ 1), 1024 + row, 2048 + (tdev % 2) * 1024 + row))
    src_ref[...] = jnp.where(mine, src, 0)
    own_ref[...] = jnp.where(mine & (tdev == j), row, -1)
    part_ref[...] = jnp.where(mine & (tdev == (j ^ 1)), row, -1)
    cross = mine & ((tdev // 2) != (j // 2))
    ind = jnp.where(cross, 1.0, 0.0).astype(F32)
    upper = jnp.where(lax.broadcasted_iota(I32, (256, 256), 0) < lax.broadcasted_iota(I32, (256, 256), 1), 1.0, 0.0).astype(BF16)
    within = jnp.dot(ind.astype(BF16), upper, preferred_element_type=F32)
    count = jnp.sum(ind, axis=1, keepdims=True)
    base = jnp.zeros((1, 1), F32)
    rows = []
    for e in range(8):
        rows.append(base)
        base = base + count[e:e + 1]
    xpos = jnp.where(cross, (within + jnp.concatenate(rows, axis=0)).astype(I32), -1)
    xpos_ref[...] = xpos
    xpos_t = jnp.transpose(xpos.astype(F32)).astype(I32)
    tok_t = jnp.transpose(((tdev % 2) * 1024 + row + 1).astype(F32)).astype(I32)
    gate_ref[...] = jnp.transpose(gate)
    lane = lax.broadcasted_iota(I32, (256, cap_r), 1)
    acc = jnp.zeros((1, cap_r), I32)
    for e in range(8):
        acc = acc + jnp.sum(jnp.where(xpos_t[:, e:e + 1] == lane, tok_t[:, e:e + 1], 0), axis=0, keepdims=True)
    xrow_ref[...] = acc - 1


def route(cap_r, sel_all, gate_two):
    slot = jax.ShapeDtypeStruct((8, 256), I32)
    return pl.pallas_call(
        functools.partial(route_kernel, cap_r),
        out_shape=(slot, slot, slot, slot, jax.ShapeDtypeStruct((1, cap_r), I32), jax.ShapeDtypeStruct((256, 8), F32)),
        in_specs=[VM, VM],
        out_specs=(VM,) * 6,
        name="route",
    )(sel_all, gate_two)


def gather_kernel(chunks, x_ref, part_ref, list_ref, psem, ssem, rsem, fsem, gsem):
    pod, i, j = coords()
    partner, across = (pod, i, j ^ 1), (pod, i, j ^ 2)
    core = lax.rem(j, 2)
    meet([partner, across])
    n = x_ref.shape[0] // chunks
    sends = []
    for k in range(chunks):
        rows = pl.ds(k * n, n)
        c = pltpu.make_async_remote_copy(x_ref.at[rows], list_ref.at[core, rows], ssem.at[k], rsem.at[k], device_id=across, device_id_type=MESH)
        c.start()
        sends.append(c)
    pcopy = pltpu.make_async_remote_copy(x_ref, part_ref, psem.at[0], psem.at[1], device_id=partner, device_id_type=MESH)
    pcopy.start()
    forwards = []
    for k in range(chunks):
        rows = pl.ds(k * n, n)
        sends[k].wait_recv()
        f = pltpu.make_async_remote_copy(list_ref.at[core, rows], list_ref.at[core, rows], fsem.at[k], gsem.at[k], device_id=partner, device_id_type=MESH)
        f.start()
        forwards.append(f)
    pcopy.wait()
    for k in range(chunks):
        sends[k].wait_send()
        forwards[k].wait()


def gather(x, chunks=8):
    n, d = x.shape
    return pl.pallas_call(
        functools.partial(gather_kernel, chunks),
        out_shape=(jax.ShapeDtypeStruct((n, d), BF16), jax.ShapeDtypeStruct((2, n, d), BF16)),
        in_specs=[ANY],
        out_specs=(ANY, ANY),
        scratch_shapes=[pltpu.SemaphoreType.DMA((2,))] + [pltpu.SemaphoreType.DMA((chunks,))] * 4,
        compiler_params=pltpu.CompilerParams(collective_id=1, has_side_effects=True),
        name="gather",
    )(x)


def gelu(v):
    return 0.5 * v * (1.0 + jnp.tanh(0.7978845608028654 * (v + 0.044715 * (v * v * v))))


def ffn_kernel(src_ref, x_ref, part_ref, list_ref, gate_ref, win_ref, wout_ref, q_ref, stage, table, rows32, rows16, acc, sem):
    e, f = pl.program_id(0), pl.program_id(1)

    @pl.when((e == 0) & (f == 0))
    def _():
        copies = []
        for k, ref in enumerate((x_ref, part_ref, list_ref.at[0], list_ref.at[1])):
            c = pltpu.make_async_copy(ref, stage.at[k], sem.at[k])
            c.start()
            copies.append(c)
        for k in range(4):
            copies[k].wait()

            @pl.loop(0, 1024 // 128)
            def _(b):
                for s in range(8):
                    piece = stage[k, pl.ds(b * 128, 128), s * 128:(s + 1) * 128].astype(F32)
                    table[pl.ds((k * 1024 + b * 128) * 8 + s, 128, 8), :] = piece

    @pl.when(f == 0)
    def _():
        @pl.loop(0, 256 // 16)
        def _(b):
            for u in range(16):
                r = b * 16 + u
                idx = src_ref[e, r]
                rows32[pl.ds(pl.multiple_of(r * 8, 8), 8), :] = table[pl.ds(pl.multiple_of(idx * 8, 8), 8), :]

        for s in range(8):
            rows16[:, s * 128:(s + 1) * 128] = rows32[pl.ds(s, 256, 8), :].astype(BF16)

    hidden = jnp.dot(rows16[...], win_ref[0], preferred_element_type=F32)
    hidden = gelu(hidden).astype(BF16)
    out = jnp.dot(hidden, wout_ref[0], preferred_element_type=F32)

    @pl.when(f == 0)
    def _():
        acc[...] = out

    @pl.when(f > 0)
    def _():
        acc[...] += out

    @pl.when(f == pl.num_programs(1) - 1)
    def _():
        cols = gate_ref[...]
        lane = lax.broadcasted_iota(I32, cols.shape, 1)
        g = jnp.sum(jnp.where(lane == e, cols, 0.0), axis=1, keepdims=True)
        q_ref[0] = (g * acc[...]).astype(BF16)


def ffn(src, x, part, lists, gate_t, w_in, w_out, tile=1024):
    e, d, ff = w_in.shape
    return pl.pallas_call(
        ffn_kernel,
        out_shape=jax.ShapeDtypeStruct((e, 256, d), BF16),
        grid=(e, ff // tile),
        in_specs=[SM, ANY, ANY, ANY, VM,
                  pl.BlockSpec((1, d, tile), lambda a, b: (a, 0, b)),
                  pl.BlockSpec((1, tile, d), lambda a, b: (a, b, 0))],
        out_specs=pl.BlockSpec((1, 256, d), lambda a, b: (a, 0, 0)),
        scratch_shapes=[pltpu.VMEM((4, 1024, d), BF16), pltpu.VMEM((4096 * 8, 128), F32), pltpu.VMEM((256 * 8, 128), F32),
                        pltpu.VMEM((256, d), BF16), pltpu.VMEM((256, d), F32), pltpu.SemaphoreType.DMA((4,))],
        compiler_params=pltpu.CompilerParams(dimension_semantics=("arbitrary", "arbitrary"), vmem_limit_bytes=56 * 2**20),
        cost_estimate=pl.CostEstimate(flops=4 * e * 256 * d * ff, bytes_accessed=4 * e * d * ff, transcendentals=0),
        name="ffn",
    )(src, x, part, lists, gate_t, w_in, w_out)


def one_hot(index_row, n):
    return jnp.where(lax.broadcasted_iota(I32, (n, index_row.shape[1]), 0) == index_row, 1.0, 0.0).astype(BF16)


def combine_kernel(cap, chunks, x_ref, q_ref, xpos_ref, own_ref, part_ref, xrow_ref, y_ref,
                   total, pq, prow, slist, rlist, xrows, psem, ssem, rsem, fsem, gsem, hsem):
    pod, i, j = coords()
    partner, across = (pod, i, j ^ 1), (pod, i, j ^ 2)
    core = lax.rem(j, 2)
    n = cap // chunks
    meet([partner, across])
    remote = functools.partial(pltpu.make_async_remote_copy, device_id_type=MESH)
    first = [
        remote(part_ref, prow, psem.at[0], psem.at[1], device_id=partner),
        remote(q_ref, pq, psem.at[2], psem.at[3], device_id=partner),
        remote(xrow_ref, xrows.at[0], psem.at[4], psem.at[5], device_id=across),
    ]
    for c in first:
        c.start()

    sends = [remote(slist.at[pl.ds(k * n, n)], rlist.at[0, pl.ds(k * n, n)], ssem.at[k], rsem.at[k], device_id=across) for k in range(chunks)]
    for k in range(chunks):
        @pl.loop(0, 4)
        def _(b):
            cols = pl.ds(pl.multiple_of(b * 256, 256), 256)
            acc = jnp.zeros((n, 256), F32)
            for e in range(8):
                acc = acc + jnp.dot(one_hot(xpos_ref[e:e + 1, :] - k * n, n), q_ref[e, :, cols], preferred_element_type=F32)
            slist[pl.ds(k * n, n), cols] = acc.astype(BF16)
        if k > 0:
            sends[k - 1].start()

    def add(rows, value_of, init=False):
        mats = None

        @pl.loop(0, 4)
        def _(b):
            cols = pl.ds(pl.multiple_of(b * 256, 256), 256)
            acc = x_ref[:, cols].astype(F32) if init else total[:, cols]
            for m, r in enumerate(rows):
                acc = acc + jnp.dot(one_hot(r, 1024), value_of(m, cols), preferred_element_type=F32)
            total[:, cols] = acc

    add([own_ref[e:e + 1, :] for e in range(4)], lambda m, cols: q_ref[m, :, cols], init=True)
    sends[chunks - 1].start()
    add([own_ref[e:e + 1, :] for e in range(4, 8)], lambda m, cols: q_ref[4 + m, :, cols])
    first[0].wait()
    first[1].wait()
    add([prow[e:e + 1, :] for e in range(4)], lambda m, cols: pq[m, :, cols])
    add([prow[e:e + 1, :] for e in range(4, 8)], lambda m, cols: pq[4 + m, :, cols])

    first[2].wait()
    pass_rows = remote(xrows.at[0], xrows.at[1], hsem.at[0], hsem.at[1], device_id=partner)
    pass_rows.start()
    forwards = []
    for k in range(chunks):
        rows = pl.ds(k * n, n)
        sends[k].wait_recv()
        f = remote(rlist.at[0, rows], rlist.at[1, rows], fsem.at[k], gsem.at[k], device_id=partner)
        f.start()
        forwards.append(f)
        add([xrows[0, :, k * n:(k + 1) * n] - core * 1024], lambda m, cols: rlist[0, rows, cols])
    pass_rows.wait()
    for k in range(chunks):
        rows = pl.ds(k * n, n)
        forwards[k].wait()
        add([xrows[1, :, k * n:(k + 1) * n] - core * 1024], lambda m, cols: rlist[1, rows, cols])
    for k in range(chunks):
        sends[k].wait_send()
    y_ref[...] = total[...].astype(BF16)


def combine(x, q, xpos, own, part, xrow, chunks=4):
    n, d = x.shape
    cap = xrow.shape[1]
    return pl.pallas_call(
        functools.partial(combine_kernel, cap, chunks),
        out_shape=jax.ShapeDtypeStruct((n, d), BF16),
        in_specs=[VM] * 6,
        out_specs=VM,
        scratch_shapes=[pltpu.VMEM((n, d), F32), pltpu.VMEM((8, 256, d), BF16), pltpu.VMEM((8, 256), I32),
                        pltpu.VMEM((cap, d), BF16), pltpu.VMEM((2, cap, d), BF16), pltpu.VMEM((2, 1, cap), I32),
                        pltpu.SemaphoreType.DMA((6,))] + [pltpu.SemaphoreType.DMA((chunks,))] * 4 + [pltpu.SemaphoreType.DMA((2,))],
        compiler_params=pltpu.CompilerParams(collective_id=2, has_side_effects=True, vmem_limit_bytes=56 * 2**20),
        name="combine",
    )(x, q, xpos, own, part, xrow)


def solution(mesh):
    row_spec = P(("pod", "data", "expert"), None)
    slot_spec = P(("pod", "expert"), "data")
    weight_spec = P("expert", None, None)

    def local_fn(x, sel, gate, w_in, w_out):
        sel_all, gate_two = share(sel, gate)
        src, xpos, own, part, xrow, gate_t = route(1024, sel_all, gate_two)
        part_x, lists = gather(x)
        q = ffn(src, x, part_x, lists, gate_t, w_in, w_out)
        return combine(x, q, xpos, own, part, xrow)

    return jax.shard_map(local_fn, mesh=mesh, in_specs=(row_spec, slot_spec, slot_spec, weight_spec, weight_spec), out_specs=row_spec, check_vma=False)
```

time: 421 us -> 205 us (0.49)
  Pallas kernels: 0 us -> 201 us
  blocking collectives: 116 us -> 0 us
  local copies, waits for them, and re-layouts: 104 us -> 3.08 us
  waiting for transfers between devices: 90.5 us -> 0 us
  matrix products: 58.4 us -> 0 us
  other arithmetic: 38.9 us -> 0 us
  starting transfers between devices: 11.7 us -> 0 us
    pallas_call x0 -> x5, Pallas kernels: none -> 201 us  [the longest x1 78.8 us: ffn(): pl.pallas_call(ffn_kernel, out_shape=jax.ShapeDtypeStruct((e, 256, d), BF...]
    all_to_all x4 -> x0, blocking collectives: 116 us -> none  [the longest x3 110 us: exchange(): buffer = lax.all_to_all(buffer, 'expert', 1, 1, tiled=True)]
    all_to_all x2 -> x0, waiting for transfers between devices: 90.5 us -> none  [exchange(): return lax.all_to_all(buffer, 'data', 0, 0, tiled=True)]
    gather x17 -> x0, local copies, waits for them, and re-layouts: 89.9 us -> none  [the longest x11 49.8 us: local_fn(): first_pos = jnp.searchsorted(sorted_src, sorted_src, side='left')]
    dot_general x2 -> x0, matrix products: 58.4 us -> none  [the longest x1 29.3 us: local_fn(): jnp.einsum('ecf,efd->ecd', hidden, w_out, preferred_element_type=jnp.floa...]
    scatter-add x1 -> x0, other arithmetic: 22.2 us -> none  [local_fn(): jax.ops.segment_sum(returned.reshape(buf_size, d_model).astype(jnp.float3...]
    all_to_all x2 -> x0, starting transfers between devices: 11.7 us -> none  [exchange(): return lax.all_to_all(buffer, 'data', 0, 0, tiled=True)]
    scatter x2 -> x0, local copies, waits for them, and re-layouts: 8.63 us -> none  [the longest x1 4.32 us: local_fn(): jnp.full(buf_size, slots, jnp.int32).at[buf_pos]]
  transfers between devices with their start and end apart: 2 -> 0, of which waited for: 2 -> 0; matrix products, arithmetic and copies ran while one was open for 1% -> 0% of each run, Pallas kernels for 0% -> 0%
where the time goes in v1:
time: 205 us
  Pallas kernels  201 us (98%)
  local copies, waits for them, and re-layouts  3.08 us (2%)
    pallas_call x1, Pallas kernels, ffn(): pl.pallas_call(ffn_kernel, out_shape=jax.ShapeDtypeStruct((e, 256, d), BF...  78.8 us
    pallas_call x1, Pallas kernels, combine(): pl.pallas_call(functools.partial(combine_kernel, cap, chunks), out_shape=...  62.1 us
    pallas_call x1, Pallas kernels, gather(): pl.pallas_call(functools.partial(gather_kernel, chunks), out_shape=(jax.S...  49.1 us
    pallas_call x1, Pallas kernels, share(): pl.pallas_call(share_kernel, out_shape=(jax.ShapeDtypeStruct((8, e, c), I...  8.08 us

profile of v1, /device:TPU:0, one launch (start us, length us, event | category | flops | bytes accessed | tf_op | source)
XLA Modules:
  0.0 204.5 jit_solution(8363251262716460255)
XLA Ops:
  0.0 8.1 %share.1 = (s32[8,8,128]{2,1,0:T(8,128)}, f32[2,8,128]{2,1,0:T(8,128)}) custom-call(s32[8,128]{1,0:T(8,128)} %sel_ref.1, f32[8,128]{1,0:T(8,128)} %gate_ref.1), custom_call_target="tpu_custom_call" | custom-call | tf_op jit(solution)/shard_map/share/pallas_call | solution.py:47
  8.1 3.2 %route.1 = (s32[8,256]{1,0:T(8,128)}, s32[8,256]{1,0:T(8,128)}, s32[8,256]{1,0:T(8,128)}, s32[8,256]{1,0:T(8,128)}, s32[1,1024]{1,0:T(1,128)}, /*index=5*/f32[256,8]{1,0:T(8,128)}) custom-call(s32[8,8,128]{2,1,0:T(8,128)} %get-tuple-element.15.sel_all, f32[2,8,128]{2,1,0:T(8,128)} %get-tuple-element.16.gate_two), custom_call_target="tpu_custom_call" | custom-call | tf_op jit(solution)/shard_map/route/pallas_call | solution.py:94
  11.3 49.1 %gather.1 = (bf16[1024,1024]{1,0:T(8,128)(2,1)}, bf16[2,1024,1024]{2,1,0:T(8,128)(2,1)}) custom-call(bf16[1024,1024]{1,0:T(8,128)(2,1)} %x_ref.5), custom_call_target="tpu_custom_call" | custom-call | tf_op jit(solution)/shard_map/gather/pallas_call | solution.py:132
  60.5 78.8 %ffn.1.q_ref = bf16[8,256,1024]{2,1,0:T(8,128)(2,1)} custom-call(s32[8,256]{1,0:T(8,128)} %get-tuple-element.17.src_ref, bf16[1024,1024]{1,0:T(8,128)(2,1)} %x_ref.5, bf16[1024,1024]{1,0:T(8,128)(2,1)} %get-tuple-element.18.part_ref, bf16[2,1024,1024]{2,1,0:T(8,128)(2,1)} %get-tuple-element.19.list_ref, f32[256,8]{1,0:T(8,128)} %get-tuple-element.20.gate_ref, ...), custom_call_target="tpu_custom_call" | custom-call | flops 34359738368 | bytes 134217728 | tf_op jit(solution)/shard_map/ffn/pallas_call | solution.py:200
  139.3 62.1 %combine.1 = bf16[1024,1024]{1,0:T(8,128)(2,1)} custom-call(bf16[1024,1024]{1,0:T(8,128)(2,1)} %x_ref.5, bf16[8,256,1024]{2,1,0:T(8,128)(2,1)} %ffn.1.q_ref, s32[8,256]{1,0:T(8,128)} %get-tuple-element.21.xpos_ref, s32[8,256]{1,0:T(8,128)} %get-tuple-element.22.own_ref, s32[8,256]{1,0:T(8,128)} %get-tuple-element.23.part_ref, ...), custom_call_target="tpu_custom_call" | custom-call | tf_op jit(solution)/shard_map/combine/pallas_call | solution.py:291
  201.5 3.1 %copy.7 = bf16[1024,1024]{1,0:T(8,128)(2,1)} copy(bf16[1024,1024]{1,0:T(8,128)(2,1)} %combine.1) | data formatting | bytes 4194304

commit v2 on v0

v2 whole, which is shorter than its diff:
```python
import functools

import jax
import jax.numpy as jnp
from jax import lax
from jax.experimental import pallas as pl
from jax.experimental.pallas import tpu as pltpu
from jax.sharding import PartitionSpec as P

MESH = pl.DeviceIdType.MESH
VM = pl.BlockSpec(memory_space=pltpu.VMEM)
SM = pl.BlockSpec(memory_space=pltpu.SMEM)
ANY = pl.BlockSpec(memory_space=pl.ANY)
F32, BF16, I32 = jnp.float32, jnp.bfloat16, jnp.int32

LANES, SLOTS, ROWS = 128, 256, 1024
PLANS = ((208, 256, 640, 6, 4), (256, 512, 1024, 3, 4))


def coords():
    return lax.axis_index("pod"), lax.axis_index("data"), lax.axis_index("expert")


def meet(peers):
    barrier = pltpu.get_barrier_semaphore()
    for peer in peers:
        pl.semaphore_signal(barrier, inc=1, device_id=peer, device_id_type=MESH)
    pl.semaphore_wait(barrier, len(peers))


def iota(shape, axis):
    return lax.broadcasted_iota(I32, shape, axis)


def where01(mask):
    return jnp.where(mask, 1.0, 0.0).astype(F32)


def share_kernel(sel_ref, gate_ref, sel_all, gate_two, send, recv, gsem):
    pod, i, j = coords()
    peers = [(pod, lax.rem(i + di, 2), lax.rem(j + dj, 4)) for di in range(2) for dj in range(4) if (di, dj) != (0, 0)]
    meet(peers)
    me = i * 4 + j
    sel_all[me] = sel_ref[...]
    gate_two[i] = gate_ref[...]
    copies = []
    for k, peer in enumerate(peers):
        copies.append(pltpu.make_async_remote_copy(sel_ref, sel_all.at[me], send.at[k], recv.at[k], device_id=peer, device_id_type=MESH))
    copies.append(pltpu.make_async_remote_copy(gate_ref, gate_two.at[i], gsem.at[0], gsem.at[1], device_id=(pod, 1 - i, j), device_id_type=MESH))
    for c in copies:
        c.start()
    for c in copies:
        c.wait()


def share(sel, gate):
    e, c = sel.shape
    return pl.pallas_call(
        share_kernel,
        out_shape=(jax.ShapeDtypeStruct((8, e, c), I32), jax.ShapeDtypeStruct((2, e, c), F32)),
        in_specs=[VM, VM],
        out_specs=(VM, VM),
        scratch_shapes=[pltpu.SemaphoreType.DMA((7,)), pltpu.SemaphoreType.DMA((7,)), pltpu.SemaphoreType.DMA((2,))],
        compiler_params=pltpu.CompilerParams(collective_id=0, has_side_effects=True),
        name="share",
    )(sel, gate)


def route_kernel(sel_all, gate_two, tok_ref, place_ref, lrow_ref, flag_ref, gate_ref, xpos_ref, own_ref, part_ref, xrow_ref, pos_scr):
    _, i, j = coords()
    chip = j // 2

    pos, tot = [], []
    for X in range(2):
        his, los = [], []
        for d in (2 * X, 2 * X + 1, 4 + 2 * X, 5 + 2 * X):
            for e in range(8):
                r = sel_all[d, e:e + 1, :]
                his.append(where01(iota((64, LANES), 0) == r // LANES).astype(BF16))
                los.append(where01(iota((LANES, LANES), 0) == r % LANES).astype(BF16))
        hi = jnp.concatenate(his, axis=1)
        lo = jnp.concatenate(los, axis=1)
        counts = lax.dot_general(hi, lo, (((1,), (1,)), ((), ())), preferred_element_type=F32)
        need = where01(counts > 0.5)
        upper = where01(iota((LANES, LANES), 0) < iota((LANES, LANES), 1)).astype(BF16)
        r64, c64 = iota((64, 64), 0), iota((64, 64), 1)
        lower = where01((c64 < r64) & (c64 // 8 == r64 // 8)).astype(BF16)
        need16 = need.astype(BF16)
        before = jnp.dot(need16, upper, preferred_element_type=F32)
        offset = jnp.sum(jnp.dot(lower, need16, preferred_element_type=F32), axis=1, keepdims=True)
        pos.append(jnp.where(need > 0.5, before + offset, -1.0).astype(I32))
        per_dev = jnp.sum(jnp.dot(where01(iota((8, 64), 0) == iota((8, 64), 1) // 8).astype(BF16), need16, preferred_element_type=F32), axis=1, keepdims=True)
        dev = iota((8, 1), 0)
        tot.append(jnp.where((dev % 4) // 2 != X, per_dev, 0.0))
    longest = jnp.max(jnp.maximum(tot[0], tot[1]))

    pos_scr[...] = jnp.where(chip == 0, pos[0], pos[1])
    mine_pos = pos_scr[pl.ds(pl.multiple_of(i * 32, 32), 32), :]
    block = iota((32, LANES), 0)
    tdev = block // 8
    row = (block % 8) * LANES + iota((32, LANES), 1)
    place_ref[...] = jnp.where(tdev == j, row, jnp.where(tdev == (j ^ 1), ROWS + row, 2048 + (tdev % 2) * ROWS + jnp.maximum(mine_pos, 0)))

    pos_scr[...] = jnp.where(chip == 0, pos[1], pos[0])
    out_pos = pos_scr[pl.ds(pl.multiple_of((i * 4 + j) * 8, 8), 8), :]
    out_t = jnp.transpose(out_pos.astype(F32)).astype(I32)
    lane = iota((LANES, ROWS), 1)
    acc = jnp.zeros((LANES, ROWS), I32)
    for h in range(8):
        acc = acc + jnp.where(out_t[:, h:h + 1] == lane, iota((LANES, 1), 0) + h * LANES, 0)
    lrow_ref[...] = jnp.sum(acc, axis=0, keepdims=True)

    sel = jnp.concatenate([sel_all[j], sel_all[4 + j]], axis=1)
    gate = jnp.concatenate([gate_two[0], gate_two[1]], axis=1)
    tdev = (sel // ROWS) % 4
    row = sel % ROWS
    mine = (sel // 4096) == i
    cross = mine & ((tdev // 2) != chip)
    upper = where01(iota((SLOTS, SLOTS), 0) < iota((SLOTS, SLOTS), 1)).astype(BF16)
    rank = jnp.dot(where01(mine).astype(BF16), upper, preferred_element_type=F32).astype(I32)
    rank = jnp.where(mine, rank, -1)
    amount = jnp.sum(where01(mine), axis=1, keepdims=True)
    xrank = jnp.dot(where01(cross).astype(BF16), upper, preferred_element_type=F32)
    xamount = jnp.sum(where01(cross), axis=1, keepdims=True)
    odd = (iota((8, 8), 0) == iota((8, 8), 1) + 1) & (iota((8, 8), 0) % 2 == 1)
    xbase = jnp.concatenate([jnp.zeros((1, 1), F32), xamount[:7]], axis=0)
    xbase = jnp.where(iota((8, 1), 0) % 2 == 1, xbase, 0.0)
    xpos = jnp.where(cross, (xrank + xbase).astype(I32), -1)
    packed = (sel % 4096) + 4096 * (xpos + 1)
    rank_t = jnp.transpose(rank.astype(F32)).astype(I32)
    packed_t = jnp.transpose(packed.astype(F32)).astype(I32)
    xpos_t = jnp.transpose(xpos.astype(F32)).astype(I32)
    far_t = jnp.transpose(((tdev % 2) * ROWS + row + 1).astype(F32)).astype(I32)
    lane = iota((SLOTS, SLOTS), 1)
    toks, columns = [], []
    for e in range(8):
        toks.append(jnp.sum(jnp.where(rank_t[:, e:e + 1] == lane, packed_t[:, e:e + 1], 0), axis=0, keepdims=True))
        gate_ref[:, e:e + 1] = jnp.sum(jnp.where(rank[e:e + 1, :] == iota((SLOTS, SLOTS), 0), gate[e:e + 1, :], 0.0), axis=1, keepdims=True)
    table = jnp.concatenate(toks, axis=0)
    tok = table % 4096
    tok_ref[...] = tok
    xpos_ref[...] = table // 4096 - 1
    there = iota((8, SLOTS), 1).astype(F32) < amount
    tdev = tok // ROWS
    own_ref[...] = jnp.where(there & (tdev == j), tok % ROWS, -1)
    part_ref[...] = jnp.where(there & (tdev == (j ^ 1)), tok % ROWS, -1)
    lane = iota((SLOTS, 512), 1)
    for g in range(4):
        acc = jnp.zeros((SLOTS, 512), I32)
        for e in (2 * g, 2 * g + 1):
            acc = acc + jnp.where(xpos_t[:, e:e + 1] == lane, far_t[:, e:e + 1], 0)
        xrow_ref[g:g + 1, :] = jnp.sum(acc, axis=0, keepdims=True) - 1

    most = jnp.zeros((8, 1), F32)
    xmost = jnp.zeros((8, 1), F32)
    for jj in range(4):
        s = jnp.concatenate([sel_all[jj], sel_all[4 + jj]], axis=1)
        far = ((s // ROWS) % 4) // 2 != jj // 2
        for h in range(2):
            m = (s // 4096) == h
            most = jnp.maximum(most, jnp.sum(where01(m), axis=1, keepdims=True))
            x = jnp.sum(where01(m & far), axis=1, keepdims=True)
            nxt = jnp.concatenate([x[1:], jnp.zeros((1, 1), F32)], axis=0)
            xmost = jnp.maximum(xmost, jnp.where(iota((8, 1), 0) % 2 == 0, x + nxt, 0.0))
    most = jnp.max(most)
    xmost = jnp.max(xmost)
    plan = jnp.int32(len(PLANS) - 1)
    for p in reversed(range(len(PLANS) - 1)):
        m, c, g = PLANS[p][:3]
        plan = jnp.where((most <= m) & (xmost <= c) & (longest <= g), p, plan)
    flag_ref[0, 0] = plan


def route(sel_all, gate_two):
    slot = jax.ShapeDtypeStruct((8, SLOTS), I32)
    return pl.pallas_call(
        route_kernel,
        out_shape=(slot, jax.ShapeDtypeStruct((32, LANES), I32), jax.ShapeDtypeStruct((1, ROWS), I32), jax.ShapeDtypeStruct((1, 1), I32),
                   jax.ShapeDtypeStruct((SLOTS, 8), F32), slot, slot, slot, jax.ShapeDtypeStruct((4, 512), I32)),
        in_specs=[VM, VM],
        out_specs=(VM, VM, VM, SM, VM, VM, VM, VM, VM),
        scratch_shapes=[pltpu.VMEM((64, LANES), I32)],
        name="route",
    )(sel_all, gate_two)


def gelu(v):
    return (0.5 * v) * (1.0 + jnp.tanh(v * (0.7978845608028654 + 0.035677408136300125 * (v * v))))


def layer_kernel(plan, tok_ref, place_ref, lrow_ref, x_ref, gate_ref, xpos_ref, own_ref, part_ref, xrow_ref, win_ref, wout_ref, y_ref,
                 xown, table, slist, rows32, tmp32, rows16, hid, acc, qq, total, rsend, rlist, prow, xrows, wi, wo, amat, src,
                 wsem, psem, lsem, qsem, rsem):
    M, cap, cap_g, depth, pieces = plan
    pod, i, j = coords()
    partner, across = (pod, i, j ^ 1), (pod, i, j ^ 2)
    core = lax.rem(j, 2)
    remote = functools.partial(pltpu.make_async_remote_copy, device_id_type=MESH)
    F = ROWS
    steps = 32

    def weights(k, slot):
        e, f = k // 4, lax.rem(k, 4)
        cols = pl.ds(pl.multiple_of(f * F, F), F)
        return (pltpu.make_async_copy(win_ref.at[e, :, cols], wi.at[slot], wsem.at[0, slot]),
                pltpu.make_async_copy(wout_ref.at[e, cols, :], wo.at[slot], wsem.at[1, slot]))

    @pl.loop(0, depth)
    def _(k):
        for c in weights(k, k):
            c.start()

    meet([partner, across])
    small = [remote(part_ref, prow, psem.at[0], psem.at[1], device_id=partner),
             remote(xrow_ref, xrows.at[core], psem.at[2], psem.at[3], device_id=across)]
    for c in small:
        c.start()

    @pl.loop(0, 8)
    def _(b):
        at = pl.multiple_of(b * LANES, LANES)
        for s in range(8):
            tmp32[pl.ds(s, LANES, 8), :] = x_ref[pl.ds(at, LANES), s * LANES:(s + 1) * LANES].astype(F32)
        tiles = tmp32[...].reshape(LANES, 8, LANES).astype(BF16)
        xown[pl.ds(at, LANES)] = tiles
        table[pl.ds(at, LANES)] = tiles

    pcopy = remote(xown, table.at[pl.ds(ROWS, ROWS)], psem.at[4], psem.at[5], device_id=partner)
    n = cap_g // pieces
    base = 2048 + core * ROWS
    sends, forwards = [], []
    for k in range(pieces):
        there = table.at[pl.ds(base + k * n, n)]
        sends.append(remote(slist.at[pl.ds(k * n, n)], there, lsem.at[0, k], lsem.at[1, k], device_id=across))
        forwards.append(remote(there, there, lsem.at[2, k], lsem.at[3, k], device_id=partner))
    for k in range(pieces):
        @pl.loop(0, n // 16)
        def _(b):
            tiles = [xown[lrow_ref[0, k * n + b * 16 + u]] for u in range(16)]
            for u, tile in enumerate(tiles):
                slist[k * n + b * 16 + u] = tile

        if k == 0:
            pcopy.start()
        else:
            sends[k - 1].start()
    total[...] = x_ref[...].astype(F32)
    sends[pieces - 1].start()
    @pl.loop(0, 8)
    def _(e):
        @pl.loop(0, M // 16)
        def _(b):
            for u in range(16):
                tok = tok_ref[e, b * 16 + u]
                src[e, b * 16 + u] = place_ref[tok >> 7, tok & (LANES - 1)]

    small[1].wait()
    pass_rows = remote(xrows.at[core], xrows.at[core], psem.at[6], psem.at[7], device_id=partner)
    pass_rows.start()
    for k in range(pieces):
        sends[k].wait_recv()
        forwards[k].start()
    small[0].wait()
    pass_rows.wait()
    pcopy.wait()
    for k in range(pieces):
        sends[k].wait_send()
        forwards[k].wait()

    def fetch(e, slot, f):
        at = pl.multiple_of(jnp.minimum(f * 64, M - 64), 16)
        for v in range(0, 64, 16):
            tiles = [table[src[e, at + v + u]].astype(F32) for u in range(16)]
            for u, tile in enumerate(tiles):
                rows32[(v + u) * 8:(v + u + 1) * 8, :] = tile
        for s in range(8):
            rows16[slot, pl.ds(at, 64), s * LANES:(s + 1) * LANES] = rows32[pl.ds(s, 64, 8), :].astype(BF16)

    @pl.loop(0, 4)
    def _(f):
        fetch(0, 0, f)

    def qcopy(g):
        return remote(qq.at[g, pl.ds(0, 2 * M)], qq.at[g, pl.ds(2 * M, 2 * M)], qsem.at[0, g], qsem.at[1, g], device_id=partner)

    def xcopy(g):
        return remote(rsend.at[g], rlist.at[g, pl.ds(core * cap, cap)], rsem.at[0, g], rsem.at[1, g], device_id=across)

    def xpass(g):
        there = rlist.at[g, pl.ds(core * cap, cap)]
        return remote(there, there, rsem.at[2, g], rsem.at[3, g], device_id=partner)

    def pair(ref, g):
        return jnp.concatenate([ref[pl.ds(2 * g, 1), :][:, :M], ref[pl.ds(2 * g + 1, 1), :][:, :M]], axis=1)

    def add(rows, ref, g):
        k = rows.shape[1]
        for b in range(4):
            amat[b * SLOTS:(b + 1) * SLOTS, :k] = where01(iota((SLOTS, k), 0) + b * SLOTS == rows).astype(BF16)

        @pl.loop(0, 4)
        def _(b):
            cols = pl.ds(pl.multiple_of(b * SLOTS, SLOTS), SLOTS)
            total[:, cols] += jnp.dot(amat[:, :k], ref[g, :, cols], preferred_element_type=F32)

    def add_chip(g):
        qcopy(g).wait_recv()
        add(jnp.concatenate([pair(own_ref, g), pair(prow, g)], axis=1), qq, g)

    def take_far(g):
        xcopy(g).wait_recv()
        xpass(g).start()

    def add_far(g):
        xpass(g).wait_recv()
        add(jnp.concatenate([xrows[0, pl.ds(g, 1), :][:, :cap], xrows[1, pl.ds(g, 1), :][:, :cap]], axis=1) - core * ROWS, rlist, g)

    @pl.loop(0, 4)
    def _(g):
        @pl.loop(0, 8)
        def _(t):
            k = g * 8 + t
            e = k // 4
            f = lax.rem(k, 4)
            cur = lax.rem(e, 2)
            slot = lax.rem(k, depth)
            for c in weights(k, slot):
                c.wait()
            fetch(jnp.minimum(e + 1, 7), 1 - cur, f)
            xs = rows16[cur]
            for s in range(4):
                u = jnp.dot(xs, wi[slot, :, s * SLOTS:(s + 1) * SLOTS], preferred_element_type=F32)
                hid[:, s * SLOTS:(s + 1) * SLOTS] = gelu(u).astype(BF16)
            out = jnp.dot(hid[...], wo[slot], preferred_element_type=F32)
            acc[...] = jnp.where(f == 0, out, acc[...] + out)

            @pl.when(k + depth < steps)
            def _():
                for c in weights(k + depth, slot):
                    c.start()

            @pl.when(f == 3)
            def _():
                cols = gate_ref[...]
                weight = jnp.sum(jnp.where(iota(cols.shape, 1) == e, cols, 0.0), axis=1, keepdims=True)[:M]
                qq[g, pl.ds(pl.multiple_of(cur * M, 16), M), :] = (weight * acc[...]).astype(BF16)

        amat[:cap, :2 * M] = where01(iota((cap, 2 * M), 0) == pair(xpos_ref, g)).astype(BF16)

        @pl.loop(0, 4)
        def _(b):
            cols = pl.ds(pl.multiple_of(b * SLOTS, SLOTS), SLOTS)
            rsend[g, :, cols] = jnp.dot(amat[:cap, :2 * M], qq[g, :2 * M, cols], preferred_element_type=F32).astype(BF16)

        qcopy(g).start()

        @pl.when(g >= 2)
        def _():
            take_far(g - 2)

        @pl.when(g == 0)
        def _():
            xcopy(g).start()

        @pl.when(g >= 1)
        def _():
            k = 4 * M
            rows = jnp.concatenate([pair(own_ref, g - 1), pair(prow, g - 1)], axis=1)
            for b in range(4):
                amat[b * SLOTS:(b + 1) * SLOTS, :k] = where01(iota((SLOTS, k), 0) + b * SLOTS == rows).astype(BF16)
            xcopy(g).start()
            qcopy(g - 1).wait_recv()

            @pl.loop(0, 4)
            def _(b):
                cols = pl.ds(pl.multiple_of(b * SLOTS, SLOTS), SLOTS)
                total[:, cols] += jnp.dot(amat[:, :k], qq[g - 1, :, cols], preferred_element_type=F32)

        @pl.when(g >= 3)
        def _():
            add_far(g - 3)

    take_far(2)
    add_chip(3)
    add_far(1)
    add_far(2)
    take_far(3)
    add_far(3)
    for g in range(4):
        qcopy(g).wait_send()
        xcopy(g).wait_send()
        xpass(g).wait_send()
    y_ref[...] = total[...].astype(BF16)


def layer(index, tok, place, lrow, x, gate_t, xpos, own, part, xrow, w_in, w_out):
    plan = PLANS[index]
    M, cap, cap_g, depth, pieces = plan
    n, d = x.shape
    e, _, ff = w_in.shape
    dma = pltpu.SemaphoreType.DMA
    return pl.pallas_call(
        functools.partial(layer_kernel, plan),
        out_shape=jax.ShapeDtypeStruct((n, d), BF16),
        in_specs=[SM, SM, SM, VM, VM, VM, VM, VM, VM, ANY, ANY],
        out_specs=VM,
        scratch_shapes=[pltpu.VMEM((n, 8, LANES), BF16), pltpu.VMEM((3072 + cap_g, 8, LANES), BF16), pltpu.VMEM((cap_g, 8, LANES), BF16),
                        pltpu.VMEM((64 * 8, LANES), F32), pltpu.VMEM((LANES * 8, LANES), F32), pltpu.VMEM((2, M, d), BF16),
                        pltpu.VMEM((M, ROWS), BF16), pltpu.VMEM((M, d), F32), pltpu.VMEM((4, 4 * M, d), BF16), pltpu.VMEM((n, d), F32),
                        pltpu.VMEM((4, cap, d), BF16), pltpu.VMEM((4, 2 * cap, d), BF16), pltpu.VMEM((8, SLOTS), I32), pltpu.VMEM((2, 4, 512), I32),
                        pltpu.VMEM((depth, d, ROWS), BF16), pltpu.VMEM((depth, ROWS, d), BF16), pltpu.VMEM((n, max(4 * M, 2 * cap)), BF16), pltpu.SMEM((8, SLOTS), I32),
                        dma((2, depth)), dma((8,)), dma((4, pieces)), dma((2, 4)), dma((4, 4))],
        compiler_params=pltpu.CompilerParams(collective_id=1 + index, has_side_effects=True, vmem_limit_bytes=67043328),
        cost_estimate=pl.CostEstimate(flops=4 * e * M * d * ff, bytes_accessed=4 * e * d * ff, transcendentals=0),
        name="layer%d" % index,
    )(tok, place, lrow, x, gate_t, xpos, own, part, xrow, w_in, w_out)


def solution(mesh):
    row_spec = P(("pod", "data", "expert"), None)
    slot_spec = P(("pod", "expert"), "data")
    weight_spec = P("expert", None, None)

    def local_fn(x, sel, gate, w_in, w_out):
        sel_all, gate_two = share(sel, gate)
        tok, place, lrow, flag, gate_t, xpos, own, part, xrow = route(sel_all, gate_two)
        args = (tok, place, lrow, x, gate_t, xpos, own, part, xrow, w_in, w_out)
        return lax.switch(flag[0, 0], [functools.partial(layer, k) for k in range(len(PLANS))], *args)

    return jax.shard_map(local_fn, mesh=mesh, in_specs=(row_spec, slot_spec, slot_spec, weight_spec, weight_spec), out_specs=row_spec, check_vma=False)
```

time: 421 us -> 133 us (0.32)
  Pallas kernels: 0 us -> 129 us
  blocking collectives: 116 us -> 0 us
  local copies, waits for them, and re-layouts: 104 us -> 3.08 us
  waiting for transfers between devices: 90.5 us -> 0 us
  matrix products: 58.4 us -> 0 us
  other arithmetic: 38.9 us -> 0 us
  starting transfers between devices: 11.7 us -> 0 us
    pallas_call x0 -> x3, Pallas kernels: none -> 129 us  [the longest x1 115 us: layer(): pl.pallas_call(functools.partial(layer_kernel, plan), out_shape=jax.Shape...]
    all_to_all x4 -> x0, blocking collectives: 116 us -> none  [the longest x3 110 us: exchange(): buffer = lax.all_to_all(buffer, 'expert', 1, 1, tiled=True)]
    all_to_all x2 -> x0, waiting for transfers between devices: 90.5 us -> none  [exchange(): return lax.all_to_all(buffer, 'data', 0, 0, tiled=True)]
    gather x17 -> x0, local copies, waits for them, and re-layouts: 89.9 us -> none  [the longest x11 49.8 us: local_fn(): first_pos = jnp.searchsorted(sorted_src, sorted_src, side='left')]
    dot_general x2 -> x0, matrix products: 58.4 us -> none  [the longest x1 29.3 us: local_fn(): jnp.einsum('ecf,efd->ecd', hidden, w_out, preferred_element_type=jnp.floa...]
    scatter-add x1 -> x0, other arithmetic: 22.2 us -> none  [local_fn(): jax.ops.segment_sum(returned.reshape(buf_size, d_model).astype(jnp.float3...]
    all_to_all x2 -> x0, starting transfers between devices: 11.7 us -> none  [exchange(): return lax.all_to_all(buffer, 'data', 0, 0, tiled=True)]
    scatter x2 -> x0, local copies, waits for them, and re-layouts: 8.63 us -> none  [the longest x1 4.32 us: local_fn(): jnp.full(buf_size, slots, jnp.int32).at[buf_pos]]
  transfers between devices with their start and end apart: 2 -> 0, of which waited for: 2 -> 0; matrix products, arithmetic and copies ran while one was open for 1% -> 0% of each run, Pallas kernels for 0% -> 0%
where the time goes in v2:
time: 133 us
  Pallas kernels  129 us (97%)
  local copies, waits for them, and re-layouts  3.08 us (2%)
    pallas_call x1, Pallas kernels, layer(): pl.pallas_call(functools.partial(layer_kernel, plan), out_shape=jax.Shape...  115 us
    pallas_call x1, Pallas kernels, share(): pl.pallas_call(share_kernel, out_shape=(jax.ShapeDtypeStruct((8, e, c), I...  8.07 us
    pallas_call x1, Pallas kernels, route(): pl.pallas_call(route_kernel, out_shape=(slot, jax.ShapeDtypeStruct((32, L...  5.76 us
    unnamed x1, local copies, waits for them, and re-layouts  3.08 us

profile of v2, /device:TPU:0, one launch (start us, length us, event | category | flops | bytes accessed | tf_op | source)
XLA Modules:
  0.0 132.6 jit_solution(15453922749050191036)
XLA Ops:
  0.0 8.1 %share.1 = (s32[8,8,128]{2,1,0:T(8,128)}, f32[2,8,128]{2,1,0:T(8,128)}) custom-call(s32[8,128]{1,0:T(8,128)} %sel_ref.1, f32[8,128]{1,0:T(8,128)} %gate_ref.1), custom_call_target="tpu_custom_call" | custom-call | tf_op jit(solution)/shard_map/share/pallas_call | solution.py:58
  8.1 5.8 %route.1 = (s32[8,256]{1,0:T(8,128)}, s32[32,128]{1,0:T(8,128)}, s32[1,1024]{1,0:T(1,128)}, s32[1,1]{1,0:T(1,128)}, f32[256,8]{1,0:T(8,128)}, /*index=5*/s32[8,2...) custom-call(s32[8,8,128]{2,1,0:T(8,128)} %get-tuple-element.85.sel_all, ...), custom_call_target="tpu_custom_call" | custom-call | tf_op jit(solution)/shard_map/route/pallas_call | solution.py:176
  14.5 114.9 %conditional.1 = (bf16[1024,1024]{1,0:T(8,128)(2,1)}) conditional(s32[]{:T(128)} %bitcast, (s32[8,256]{1,0:T(8,128)}, s32[32,128]{1,0:T(8,128)}, s32[1,1024]{1,0:T(1,128)}, bf16[1024,1024]{1,0:T(8,128)(2,1)}, f32[256,8]{1,0:T(8,128)}, /*index=5*/s32[8,256]{1,0:T(8,128)}, s32[8,256]{1,0:T(8,128)}, s32[8,256]{1,0:T(8,128)}, s32[4,512]{1,0:T(4,128)}, ...), branch_computations={%region_0.0_spmd, %region_1.0_spmd} | conditional | flops 34359738368 | bytes 134217728 | solution.py:428
  14.6 114.7 %layer0.1 = bf16[1024,1024]{1,0:T(8,128)(2,1)} custom-call(s32[8,256]{1,0:T(8,128)} %get-tuple-element.52.tok_ref, s32[32,128]{1,0:T(8,128)} %get-tuple-element.53.place_ref, s32[1,1024]{1,0:T(1,128)} %get-tuple-element.54.lrow_ref, bf16[1024,1024]{1,0:T(8,128)(2,1)} %get-tuple-element.55.x_ref, f32[256,8]{1,0:T(8,128)} %get-tuple-element.56.gate_ref, ...), custom_call_target="tpu_custom_call" | custom-call | flops 27917287424 | bytes 134217728 | tf_op jit(solution)/shard_map/cond/branch_0_fun/layer0/pallas_call | solution.py:402
  129.5 3.1 %copy.11 = bf16[1024,1024]{1,0:T(8,128)(2,1)} copy(bf16[1024,1024]{1,0:T(8,128)(2,1)} %get-tuple-element.96) | data formatting | bytes 4194304
